TPU v7x, 32 devices: a whole 2x2x4 slice. The times are simulated.
32 devices in a mesh: fsdp: 2 (over x), context: 4 (over z), tensor: 4 (over y, core).
Axes of the slice: x: 2, y: 2, z: 4, core: 2. Of those that a mesh axis runs over, the one named last changes fastest.
Arguments:
- activations: bfloat16 [2, 2048, 1152], P('fsdp', 'context'), may hold values from -6 to 6
- positions: int32 [2, 2048], P('fsdp', 'context'), may hold values from 0 to 2047, as said below
- seg_ids: int32 [2, 2048], P('fsdp', 'context'), may hold values from 0 to 3, as said below
- norm_gains: bfloat16 [4, 1152], P(None, ('fsdp', 'context')), may hold values from 0.5 to 1.5
- head_gains: bfloat16 [2, 256], P(None, ('fsdp', 'context')), may hold values from 0.25 to 1.75
- w_query: bfloat16 [1152, 1024], P(('fsdp', 'context'), 'tensor'), may hold values from -0.1875 to 0.1875
- w_keyval: bfloat16 [1152, 512], P(('fsdp', 'context')), may hold values from -0.1875 to 0.1875
- w_out: bfloat16 [1152, 1024], P(('fsdp', 'context'), 'tensor'), may hold values from -0.1875 to 0.1875
- w_gateup: bfloat16 [1152, 2, 6912], P(('fsdp', 'context'), None, 'tensor'), may hold values from -0.1875 to 0.1875
- w_down: bfloat16 [1152, 6912], P(('fsdp', 'context'), 'tensor'), may hold values from -0.078125 to 0.078125
- cotangent: bfloat16 [2, 2048, 1152], P('fsdp', 'context'), may hold values from -6 to 6
Outputs:
- block_output: bfloat16 [2, 2048, 1152], P('fsdp', 'context')
- input_grad: bfloat16 [2, 2048, 1152], P('fsdp', 'context')
- norm_gains_grad: float32 [4, 1152], P(None, ('fsdp', 'context'))
- head_gains_grad: float32 [2, 256], P(None, ('fsdp', 'context'))
- w_query_grad: float32 [1152, 1024], P(('fsdp', 'context'), 'tensor')
- w_keyval_grad: float32 [1152, 512], P(('fsdp', 'context'))
- w_out_grad: float32 [1152, 1024], P(('fsdp', 'context'), 'tensor')
- w_gateup_grad: float32 [1152, 2, 6912], P(('fsdp', 'context'), None, 'tensor')
- w_down_grad: float32 [1152, 6912], P(('fsdp', 'context'), 'tensor')
Inputs may be any that keep to these rules, and one draw needn't show every extreme that they name: `positions`: within a sequence, a document is a run of consecutive tokens with one document number; numbers never fall along a sequence. Positions are 0 at a document's first token and rise by one from token to token inside it. The first sequence is one document. `seg_ids`: document numbers of a sequence start at 0 and never fall along it.
All inputs are finite; a program needn't handle non-finite values.
Results may differ from a plain program's by a relative error of at most 0.024.
Values may be sent and summed in bfloat16 or wider, within the bound.
A program may use at most 192 MiB of HBM per device.

v0:
```python
import jax
import jax.numpy as jnp
from jax import lax
from jax.sharding import PartitionSpec as P

HD = 256
WINDOW = 512
EPSILON = 1e-06


def from_behind(block, axis, distance):
    devices = range(lax.axis_size(axis))
    route = [(i - distance, i) for i in devices if i - distance in devices]
    return lax.ppermute(block, axis, route)


def rms_norm(values, gain):
    factor = lax.rsqrt(jnp.mean(values * values, axis=-1, keepdims=True) + EPSILON)
    return values * factor * gain


def rotate(tensor, places):
    width_all = tensor.shape[-1]
    half_width = width_all // 2
    freqs = jnp.power(10000.0, -jnp.arange(half_width, dtype=jnp.float32) * 2.0 / width_all)
    angles = places.astype(jnp.float32)[:, None] * freqs[None, :]
    cosine = jnp.cos(angles)[:, None, :]
    sine = jnp.sin(angles)[:, None, :]
    first_half = tensor[..., :half_width]
    second_half = tensor[..., half_width:]
    return jnp.concatenate(
        [first_half * cosine - second_half * sine, second_half * cosine + first_half * sine],
        axis=-1,
    )


def glu(gate_up):
    return jax.nn.gelu(gate_up[:, 0], approximate=True) * gate_up[:, 1]


def contract_last(left_side, right_side):
    return lax.dot_general(
        left_side, right_side, (((1,), (1,)), ((), ())), preferred_element_type=jnp.float32
    )


def contract_first(left_side, right_side):
    return lax.dot_general(
        left_side, right_side, (((0,), (0,)), ((), ())), preferred_element_type=jnp.float32
    )


def shards(
    activations,
    positions,
    seg_ids,
    norm_gains,
    head_gains,
    w_query,
    w_keyval,
    w_out,
    w_gateup,
    w_down,
    cotangent,
):
    tokens = activations.shape[1]
    local_heads = w_query.shape[1] // HD
    inputs = activations[0].astype(jnp.float32)
    places = positions[0]
    documents = seg_ids[0]
    gains_all, heads_all, query_all, keyval_all, out_all = (
        lax.all_gather(norm_gains, ("fsdp", "context"), axis=1, tiled=True),
        lax.all_gather(head_gains, ("fsdp", "context"), axis=1, tiled=True),
        lax.all_gather(w_query, ("fsdp", "context"), axis=0, tiled=True),
        lax.all_gather(w_keyval, ("fsdp", "context"), axis=0, tiled=True),
        lax.all_gather(w_out, ("fsdp", "context"), axis=0, tiled=True),
    )
    gains_f = gains_all.astype(jnp.float32)
    heads_f = heads_all.astype(jnp.float32)
    normed_f, input_back = jax.vjp(rms_norm, inputs, gains_f[0])
    normed = normed_f.astype(jnp.bfloat16)
    query_raw = jnp.dot(normed, query_all, preferred_element_type=jnp.float32).reshape(
        tokens, local_heads, HD
    )
    keyval_raw = jnp.dot(normed, keyval_all, preferred_element_type=jnp.float32)

    def prepare(raw_heads, head_gain):
        return rotate(rms_norm(raw_heads, head_gain), places)

    query_rot, query_back = jax.vjp(prepare, query_raw, heads_f[0])
    key_rot, key_back = jax.vjp(prepare, keyval_raw[:, None, :HD], heads_f[1])
    queries = query_rot.astype(jnp.bfloat16)
    own_keyval = jnp.concatenate([key_rot[:, 0], keyval_raw[:, HD:]], axis=1).astype(jnp.bfloat16)
    labels = jnp.stack([places, documents])
    keep_from = tokens - tokens
    left_keyval, left_labels = from_behind((own_keyval, labels), "context", 1)
    keys_all = jnp.concatenate([left_keyval, own_keyval], axis=0)
    key_places = jnp.concatenate([left_labels[0], places])
    key_documents = jnp.concatenate([left_labels[1], documents])
    has_left = lax.axis_index("context") > 0
    key_live = jnp.concatenate([jnp.full((tokens,), has_left), jnp.ones((tokens,), dtype=bool)])
    scale_factor = HD ** (-0.5)
    block_rows = 512
    block_starts = jnp.arange(tokens // block_rows) * block_rows

    def block_scores():
        spacing = places[:, None] - key_places[None, :]
        visible = (
            key_live[None, :]
            & (documents[:, None] == key_documents[None, :])
            & (spacing >= 0)
            & (spacing < WINDOW)
        )
        raw_scores = (
            jnp.einsum("qhd,kd->hqk", queries, keys_all[:, :HD], preferred_element_type=jnp.float32)
            * scale_factor
        )
        return (jnp.where(visible[None], raw_scores, -1e30), keys_all, queries)

    def forward_block(start):
        scores, near_keyval, query_block = block_scores()
        row_top = jnp.max(scores, axis=-1, keepdims=True)
        raised = jnp.exp(scores - row_top)
        row_total = jnp.sum(raised, axis=-1, keepdims=True)
        probs = raised / row_total
        mixed_block = jnp.einsum(
            "hqk,kd->qhd",
            probs.astype(jnp.bfloat16),
            near_keyval[:, HD:],
            preferred_element_type=jnp.float32,
        )
        return (mixed_block.astype(jnp.bfloat16), row_top + jnp.log(row_total))

    mixed_blocks, log_blocks = lax.map(forward_block, block_starts)
    mixed_low = mixed_blocks.reshape(tokens, local_heads * HD)
    branch = lax.psum(contract_last(mixed_low, out_all), "tensor")
    post_attn, post_attn_back = jax.vjp(rms_norm, branch, gains_f[1])
    hidden = inputs + post_attn
    normed_mlp_f, pre_mlp_back = jax.vjp(rms_norm, hidden, gains_f[2])
    normed_mlp = normed_mlp_f.astype(jnp.bfloat16)
    columns = normed_mlp
    gate_up = jnp.einsum(
        "bn,nkf->bkf",
        columns,
        lax.all_gather(w_gateup, ("fsdp", "context"), axis=0, tiled=True),
        preferred_element_type=jnp.float32,
    )
    active_f, glu_back = jax.vjp(glu, gate_up)
    active = active_f.astype(jnp.bfloat16)
    down = lax.psum(
        contract_last(
            active, lax.all_gather(w_down, ("fsdp", "context"), axis=0, tiled=True)
        ).astype(jnp.bfloat16),
        "tensor",
    ).astype(jnp.float32)
    post_mlp, post_mlp_back = jax.vjp(rms_norm, down, gains_f[3])
    result = hidden + post_mlp
    grad_out = cotangent[0].astype(jnp.float32)
    d_down, gain_post_mlp = post_mlp_back(grad_out)
    down_low = d_down.astype(jnp.bfloat16)
    columns = down_low
    d_active = jnp.dot(
        columns,
        lax.all_gather(w_down, ("fsdp", "context"), axis=0, tiled=True),
        preferred_element_type=jnp.float32,
    )
    d_gate_up = glu_back(d_active)[0].astype(jnp.bfloat16)
    d_normed_part = jnp.einsum(
        "bkf,nkf->bn",
        d_gate_up,
        lax.all_gather(w_gateup, ("fsdp", "context"), axis=0, tiled=True),
        preferred_element_type=jnp.float32,
    )
    d_normed_mlp = lax.psum(d_normed_part.astype(jnp.bfloat16), "tensor").astype(jnp.float32)
    d_hidden_norm, gain_pre_mlp = pre_mlp_back(d_normed_mlp)
    d_hidden = grad_out + d_hidden_norm
    features = normed_mlp
    grad_cols = down_low
    gate_up_term = jnp.einsum(
        "bn,bkf->nkf", features, d_gate_up, preferred_element_type=jnp.float32
    )
    down_term = contract_first(grad_cols, active)
    mlp_grads = lax.psum_scatter(
        jnp.concatenate([gate_up_term, down_term[:, None, :]], axis=1).astype(jnp.bfloat16),
        ("fsdp", "context"),
        scatter_dimension=0,
        tiled=True,
    ).astype(jnp.float32)
    d_branch, gain_post_attn = post_attn_back(d_hidden)
    branch_low = d_branch.astype(jnp.bfloat16)
    d_mixed = jnp.dot(branch_low, out_all, preferred_element_type=jnp.float32)
    d_mixed_low = d_mixed.astype(jnp.bfloat16).reshape(tokens, local_heads, HD)

    def backward_block(carry, item):
        start, log_block = item
        scores, near_keyval, query_block = block_scores()
        probs_again = jnp.exp(scores - log_block)
        d_probs = jnp.einsum(
            "qhd,kd->hqk", d_mixed_low, near_keyval[:, HD:], preferred_element_type=jnp.float32
        )
        row_inner = jnp.sum(probs_again * d_probs, axis=-1, keepdims=True)
        d_scores = (probs_again * (d_probs - row_inner)).astype(jnp.bfloat16)
        d_query_block = (
            jnp.einsum(
                "hqk,kd->qhd", d_scores, near_keyval[:, :HD], preferred_element_type=jnp.float32
            )
            * scale_factor
        )
        d_keys = (
            jnp.einsum("hqk,qhd->kd", d_scores, query_block, preferred_element_type=jnp.float32)
            * scale_factor
        )
        d_values = jnp.einsum(
            "hqk,qhd->kd",
            probs_again.astype(jnp.bfloat16),
            d_mixed_low,
            preferred_element_type=jnp.float32,
        )
        updated = carry + jnp.concatenate([d_keys, d_values], axis=1)
        return (updated, d_query_block)

    d_keyval, d_query_blocks = lax.scan(
        backward_block,
        jnp.zeros((tokens + tokens, 2 * HD), jnp.float32),
        (block_starts, log_blocks),
    )
    d_queries = d_query_blocks.reshape(tokens, local_heads, HD)
    returned = from_behind(d_keyval[:tokens].astype(jnp.bfloat16), "context", -1).astype(
        jnp.float32
    )
    own_grad = d_keyval[tokens:].at[keep_from:].add(returned)
    d_query_raw, gain_query = query_back(d_queries)
    d_query_low = d_query_raw.reshape(tokens, local_heads * HD).astype(jnp.bfloat16)
    d_normed_query, keyval_grad, gain_query_all = (
        lax.psum(contract_last(d_query_low, query_all).astype(jnp.bfloat16), "tensor").astype(
            jnp.float32
        ),
        lax.psum(own_grad.astype(jnp.bfloat16), "tensor").astype(jnp.float32),
        lax.psum(gain_query.astype(jnp.bfloat16), "tensor").astype(jnp.float32),
    )
    d_key_raw, gain_key = key_back(keyval_grad[:, None, :HD])
    d_keyval_low = jnp.concatenate([d_key_raw[:, 0], keyval_grad[:, HD:]], axis=1).astype(
        jnp.bfloat16
    )
    d_normed = d_normed_query + contract_last(d_keyval_low, keyval_all)
    d_input_norm, gain_input = input_back(d_normed)
    input_total = d_hidden + d_input_norm
    features = normed
    grad_cols = branch_low
    attn_grads = lax.psum_scatter(
        jnp.stack(
            [contract_first(features, d_query_low), contract_first(grad_cols, mixed_low)], axis=1
        ).astype(jnp.bfloat16),
        ("fsdp", "context"),
        scatter_dimension=0,
        tiled=True,
    ).astype(jnp.float32)
    keyval_term = contract_first(normed, d_keyval_low)
    gain_terms = jnp.stack([gain_input, gain_post_attn, gain_pre_mlp, gain_post_mlp])
    head_terms = jnp.stack([gain_query_all, gain_key])
    gain_grad, head_grad, keyval_weight_grad = (
        lax.psum_scatter(
            gain_terms.astype(jnp.bfloat16), ("fsdp", "context"), scatter_dimension=1, tiled=True
        ).astype(jnp.float32),
        lax.psum_scatter(
            head_terms.astype(jnp.bfloat16), ("fsdp", "context"), scatter_dimension=1, tiled=True
        ).astype(jnp.float32),
        lax.psum_scatter(
            keyval_term.astype(jnp.bfloat16), ("fsdp", "context"), scatter_dimension=0, tiled=True
        ).astype(jnp.float32),
    )
    return (
        result[None].astype(jnp.bfloat16),
        input_total[None].astype(jnp.bfloat16),
        gain_grad,
        head_grad,
        attn_grads[:, 0],
        keyval_weight_grad,
        attn_grads[:, 1],
        mlp_grads[:, :2],
        mlp_grads[:, 2],
    )


def solution(mesh):
    return jax.shard_map(
        shards,
        mesh=mesh,
        in_specs=(
            P("fsdp", "context", None),
            P("fsdp", "context"),
            P("fsdp", "context"),
            P(None, ("fsdp", "context")),
            P(None, ("fsdp", "context")),
            P(("fsdp", "context"), "tensor"),
            P(("fsdp", "context"), None),
            P(("fsdp", "context"), "tensor"),
            P(("fsdp", "context"), None, "tensor"),
            P(("fsdp", "context"), "tensor"),
            P("fsdp", "context", None),
        ),
        out_specs=(
            P("fsdp", "context", None),
            P("fsdp", "context", None),
            P(None, ("fsdp", "context")),
            P(None, ("fsdp", "context")),
            P(("fsdp", "context"), "tensor"),
            P(("fsdp", "context"), None),
            P(("fsdp", "context"), "tensor"),
            P(("fsdp", "context"), None, "tensor"),
            P(("fsdp", "context"), "tensor"),
        ),
        check_vma=False,
    )
```

profile of v0, /device:TPU:0, one launch (start us, length us, event | category | flops | bytes accessed | tf_op | source)
XLA Modules:
  0.0 1370.4 jit_solution(6977014308560481948)
XLA Ops:
  14.3 18.8 %all-gather.1 = bf16[8,32,2]{1,2,0:T(2,128)(2,1)S(1)} all-gather(bf16[1,32,2]{1,2,0:T(2,128)(2,1)} %bitcast.247), channel_id=1, replica_groups=mesh['fsdp'=2,'context'=4,'tensor'=4] {'fsdp','context'}, dimensions={0}, use_global_device_ids=true | all-gather | bytes 1152 | tf_op jit(solution)/shard_map/all_gather | solution.py:73
  33.2 27.2 %all-gather = bf16[8,144,4]{1,2,0:T(4,128)(2,1)S(1)} all-gather(bf16[1,144,4]{1,2,0:T(4,128)(2,1)} %bitcast.246), channel_id=1, replica_groups=mesh['fsdp'=2,'context'=4,'tensor'=4] {'fsdp','context'}, dimensions={0}, use_global_device_ids=true | all-gather | bytes 10368 | tf_op jit(solution)/shard_map/all_gather | solution.py:72
  62.8 32.6 %all_gather.26 = bf16[1152,256]{1,0:T(8,128)(2,1)S(1)} all-gather(bf16[144,256]{1,0:T(8,128)(2,1)} %param.20), channel_id=1, replica_groups=mesh['fsdp'=2,'context'=4,'tensor'=4] {'fsdp','context'}, dimensions={0}, use_global_device_ids=true | all-gather | bytes 663552 | tf_op jit(solution)/shard_map/all_gather | solution.py:74
  105.9 32.7 %all_gather.27 = bf16[1152,256]{1,0:T(8,128)(2,1)S(1)} all-gather(bf16[144,256]{1,0:T(8,128)(2,1)S(1)} %copy-done.37), channel_id=1, replica_groups=mesh['fsdp'=2,'context'=4,'tensor'=4] {'fsdp','context'}, dimensions={0}, use_global_device_ids=true | all-gather | bytes 663552 | tf_op jit(solution)/shard_map/all_gather | solution.py:76
  147.8 55.6 %all-reduce.15.cloned.1.call-done = f32[512,1152]{1,0:T(8,128)} async-done(((f32[512,1152]{1,0:T(8,128)}), f32[512,1152]{1,0:T(8,128)}) %all-reduce.15.cloned.1.call-update) | async-done | bytes 2359312 | tf_op jit(solution)/shard_map/psum | solution.py:136
  208.5 120.5 %all-gather.8.cloned.1.call-done = bf16[1152,2,1728]{2,0,1:T(8,128)(2,1)} async-done(((bf16[144,2,1728]{2,0,1:T(8,128)(2,1)}), bf16[1152,2,1728]{2,0,1:T(8,128)(2,1)}) %all-gather.8.cloned.1.call-update) | async-done | bytes 7962640 | tf_op jit(solution)/shard_map/all_gather | solution.py:145
  329.0 8.3 fusion.110
  342.7 58.4 %all-gather.10.cloned.1.call-done = bf16[1152,1728]{1,0:T(8,128)(2,1)} async-done(((bf16[144,1728]{1,0:T(8,128)(2,1)}), bf16[1152,1728]{1,0:T(8,128)(2,1)}) %all-gather.10.cloned.1.call-update) | async-done | bytes 3981328 | tf_op jit(solution)/shard_map/all_gather | solution.py:152
  401.1 6.3 convolution_convert_fusion.4
  408.0 35.7 %all-reduce.17.cloned.1.call-done = bf16[512,1152]{1,0:T(8,128)(2,1)} async-done(((bf16[512,1152]{1,0:T(8,128)(2,1)}), bf16[512,1152]{1,0:T(8,128)(2,1)}) %all-reduce.17.cloned.1.call-update) | async-done | bytes 1179664 | tf_op jit(solution)/shard_map/psum | solution.py:150
  448.8 11.4 multiply_bitcast_fusion
  462.0 8.1 fusion.8
  471.6 36.4 %all-reduce.19.cloned.1.call-done = bf16[512,1152]{1,0:T(8,128)(2,1)} async-done(((bf16[512,1152]{1,0:T(8,128)(2,1)}), bf16[512,1152]{1,0:T(8,128)(2,1)}) %all-reduce.19.cloned.1.call-update) | async-done | bytes 1179664 | tf_op jit(solution)/shard_map/psum | solution.py:174
  527.6 11.5 collective-permute-done.2
  544.1 7.0 psum.47
  556.0 28.6 %all-reduce.23.cloned.1.call-done = (bf16[512,1152]{1,0:T(8,128)(2,1)}, bf16[512,512]{0,1:T(8,128)(2,1)}) async-done(((bf16[512,1152]{1,0:T(8,128)(2,1)}, bf16[512,512]{0,1:T(8,128)(2,1)}), (bf16[512,1152]{1,0:T(8,128)(2,1)}, bf16[512,512]{0,1:T(8,128)(2,1)})) %all-reduce.23.cloned.1.call-update) | async-done | bytes 1703952 | tf_op jit(solution)/shard_map/psum | solution.py:235
  601.1 6.6 fusion
  607.7 9.4 convolution_convert_fusion
  617.1 7.5 pad_maximum_fusion
  624.5 27.1 %copy.35 = bf16[1152,3,1728]{2,1,0:T(4,128)(2,1)} copy(bf16[1152,3,1728]{0,2,1:T(8,128)(2,1)} %pad_maximum_fusion) | data formatting | bytes 23887872 | tf_op jit(solution)/shard_map/concatenate | solution.py:184
  659.1 59.0 %reduce-scatter.13.cloned.1.call-done = bf16[144,4]{1,0:T(8,128)(2,1)} async-done(((bf16[1152,4]{1,0:T(8,128)(2,1)}), bf16[144,4]{1,0:T(8,128)(2,1)}) %reduce-scatter.13.cloned.1.call-update) | async-done | bytes 1168
  719.6 65.5 %reduce-scatter.9.cloned.1.call-done = bf16[144,2,256]{2,0,1:T(8,128)(2,1)} async-done(((bf16[1152,2,256]{2,0,1:T(8,128)(2,1)}), bf16[144,2,256]{2,0,1:T(8,128)(2,1)}) %reduce-scatter.9.cloned.1.call-update) | async-done | bytes 147472 | tf_op jit(solution)/shard_map/reduce_scatter | solution.py:250
  786.7 65.4 %reduce-scatter.11.cloned.1.call-done = bf16[144,512]{1,0:T(8,128)(2,1)} async-done(((bf16[1152,512]{1,0:T(8,128)(2,1)}), bf16[144,512]{1,0:T(8,128)(2,1)}) %reduce-scatter.11.cloned.1.call-update) | async-done | bytes 147472 | tf_op jit(solution)/shard_map/reduce_scatter | solution.py:268
  853.7 503.4 %all-reduce.21.cloned.1.call-done = bf16[1152,3,1728]{2,1,0:T(4,128)(2,1)} async-done(((bf16[1152,3,1728]{2,1,0:T(4,128)(2,1)}), bf16[1152,3,1728]{2,1,0:T(4,128)(2,1)}) %all-reduce.21.cloned.1.call-update) | async-done | bytes 11943952
  (302 shorter events, 111.2 us)
Async XLA Ops:
  7.2 92.0 %all-gather.6.cloned.1.call-start = ((), (), s32[]{:S(2)}) async-start(), calls=%async_computation.4 | async-start | bytes 1327104 | tf_op jit(solution)/shard_map/all_gather | solution.py:75
  7.9 195.5 %all-reduce.15.cloned.1.call-start = ((), (), s32[]{:S(2)}) async-start(), calls=%async_computation.5 | async-start | bytes 4718592 | tf_op jit(solution)/shard_map/psum | solution.py:136
  8.7 130.0 %collective-permute-start.1 = (s32[2,512]{1,0:T(2,128)S(1)}, s32[2,512]{1,0:T(2,128)S(1)}, u32[]{:S(2)}, u32[]{:S(2)}) collective-permute-start(s32[2,512]{1,0:T(2,128)S(1)} %pad_add_fusion.2), channel_id=1, source_target_pairs={{0,4},{4,8},{8,12},{1,5},{5,9},{9,13},{2,6},{6,10},{10,14},{3,7},{... | collective-permute-start | bytes 12296 | tf_op jit(solution)/shard_map/ppermute | solution.py:14
  14.3 87.5 %copy-start.41 = (f32[512]{0:T(512)}, f32[512]{0:T(512)S(1)}, u32[]{:S(2)}) copy-start(f32[512]{0:T(512)S(1)} %convert_element_type.160) | copy-start | bytes 6148
  60.5 41.3 %copy-start.78 = (f32[128]{0:T(128)}, f32[128]{0:T(128)S(1)}, u32[]{:S(2)}) copy-start(f32[128]{0:T(128)S(1)} %multiply_power_fusion) | copy-start | bytes 1540
  61.1 38.1 %copy-start.47 = (f32[1152]{0:T(1024)}, f32[1152]{0:T(1024)S(1)}, u32[]{:S(2)}) copy-start(f32[1152]{0:T(1024)S(1)} %get-tuple-element.128) | copy-start | bytes 13828
  62.7 38.9 %copy-start.66 = (f32[1,256]{1,0:T(1,128)}, f32[1,256]{1,0:T(1,128)S(1)}, u32[]{:S(2)}) copy-start(f32[1,256]{1,0:T(1,128)S(1)} %get-tuple-element.154) | copy-start | bytes 3076
  101.7 37.0 %copy-start.43 = (f32[512]{0:T(512)}, f32[512]{0:T(512)S(1)}, u32[]{:S(2)}) copy-start(f32[512]{0:T(512)S(1)} %fusion.113) | copy-start | bytes 6148
  101.7 37.0 %copy-start.62 = (s32[1,512]{1,0:T(1,128)S(1)}, s32[1,512]{1,0:T(1,128)}, u32[]{:S(2)}) copy-start(s32[1,512]{1,0:T(1,128)} %param.16) | copy-start | bytes 6148
  101.7 37.0 %copy-start.72 = (s32[1,512]{1,0:T(1,128)S(1)}, s32[1,512]{1,0:T(1,128)}, u32[]{:S(2)}) copy-start(s32[1,512]{1,0:T(1,128)} %param.17) | copy-start | bytes 6148
  103.7 38.6 %copy-start.30 = (bf16[512,128]{0,1:T(8,128)(2,1)}, bf16[512,128]{0,1:T(8,128)(2,1)S(1)}, u32[]{:S(2)}) copy-start(bf16[512,128]{0,1:T(8,128)(2,1)S(1)} %get-tuple-element.141) | copy-start | bytes 393220
  103.8 34.9 %collective-permute-start = (bf16[512,512]{0,1:T(8,128)(2,1)S(1)}, bf16[512,512]{0,1:T(8,128)(2,1)}, u32[]{:S(2)}, u32[]{:S(2)}) collective-permute-start(bf16[512,512]{0,1:T(8,128)(2,1)S(1)} %pad_maximum_fusion.3), channel_id=1, source_target_pairs={{0,4},{4,8},{8,12},{1,5},{5,9},{9,13},{2,6},{6,10},{10,14},{3,7},{... | collective-permute-start | bytes 1572872 | tf_op jit(solution)/shard_map/ppermute | solution.py:14
  145.7 183.3 %all-gather.8.cloned.1.call-start = ((), (), s32[]{:S(2)}) async-start(), calls=%async_computation.6 | async-start | bytes 9289728 | tf_op jit(solution)/shard_map/all_gather | solution.py:145
  146.9 254.2 %all-gather.10.cloned.1.call-start = ((), (), s32[]{:S(2)}) async-start(), calls=%async_computation.7 | async-start | bytes 4644864 | tf_op jit(solution)/shard_map/all_gather | solution.py:152
  147.5 296.3 %all-reduce.17.cloned.1.call-start = ((), (), s32[]{:S(2)}) async-start(), calls=%async_computation.8 | async-start | bytes 2359296 | tf_op jit(solution)/shard_map/psum | solution.py:150
  208.5 128.8 %copy-start.50 = (f32[512]{0:T(512)}, f32[512]{0:T(512)S(1)}, u32[]{:S(2)}) copy-start(f32[512]{0:T(512)S(1)} %fusion.116) | copy-start | bytes 6148
  407.4 100.6 %all-reduce.19.cloned.1.call-start = ((), (), s32[]{:S(2)}) async-start(), calls=%async_computation.9 | async-start | bytes 2359296 | tf_op jit(solution)/shard_map/psum | solution.py:174
  470.1 114.4 %all-reduce.23.cloned.1.call-start = ((), (), s32[]{:S(2)}) async-start(), calls=%async_computation.15 | async-start | bytes 3407872 | tf_op jit(solution)/shard_map/psum | solution.py:235
  523.7 15.5 %collective-permute-start.2 = (bf16[512,512]{0,1:T(8,128)(2,1)S(1)}, bf16[512,512]{0,1:T(8,128)(2,1)S(1)}, u32[]{:S(2)}, u32[]{:S(2)}) collective-permute-start(bf16[512,512]{0,1:T(8,128)(2,1)S(1)} %fusion.62), channel_id=1, source_target_pairs={{4,0},{8,4},{12,8},{5,1},{9,5},{13,9},{6,2},{10,6},{14,10},{7,3},{... | collective-permute-start | bytes 1572872 | tf_op jit(solution)/shard_map/ppermute | solution.py:14
  540.2 117.6 %reduce-scatter.15.cloned.1.call-start = ((), (), s32[]{:S(2)}) async-start(), calls=%async_computation.13 | async-start | bytes 73728
  593.4 124.7 %reduce-scatter.13.cloned.1.call-start = ((), (), s32[]{:S(2)}) async-start(), calls=%async_computation.12 | async-start | bytes 331776
  596.4 188.6 %reduce-scatter.9.cloned.1.call-start = ((), (), s32[]{:S(2)}) async-start(), calls=%async_computation.10 | async-start | bytes 1327104 | tf_op jit(solution)/shard_map/reduce_scatter | solution.py:250
  597.7 254.4 %reduce-scatter.11.cloned.1.call-start = ((), (), s32[]{:S(2)}) async-start(), calls=%async_computation.11 | async-start | bytes 1327104 | tf_op jit(solution)/shard_map/reduce_scatter | solution.py:268
  601.0 756.1 %all-reduce.21.cloned.1.call-start = ((), (), s32[]{:S(2)}) async-start(), calls=%async_computation.14 | async-start | bytes 33030144
  (79 other events, 612.7 us)
Sparse Core Ops, SparseCore 0:
  10.1 43.7 all-gather.5
  145.8 57.4 all-reduce.14
  206.1 122.8 all-gather.7
  331.0 70.0 all-gather.9
  407.6 36.1 all-reduce.16
  470.2 37.7 all-reduce.18
  540.3 44.1 all-reduce.22
  593.5 62.4 reduce-scatter.14
  659.9 58.1 reduce-scatter.12
  721.3 63.6 reduce-scatter.8
  788.4 63.5 reduce-scatter.10
  856.0 501.0 all-reduce.20
where the time goes:
time: 1380 us; the launch traced here: 1370 us
  waiting for transfers between devices  1040 us (75%)
  blocking collectives  118 us (9%)
  matrix products  74.4 us (5%)
  other arithmetic  55 us (4%)
  local copies, waits for them, and re-layouts  54.9 us (4%)
  between operations  16.3 us (1%)
    unnamed x15, waiting for transfers between devices  564 us
    all_gather x1, waiting for transfers between devices, shards(): lax.all_gather(w_gateup, ('fsdp', 'context'), axis=0, tiled=True)  121 us
    reduce_scatter x1, waiting for transfers between devices, shards(): lax.psum_scatter(jnp.stack([contract_first(features, d_query_low), contra...  65.5 us
    reduce_scatter x1, waiting for transfers between devices, shards(): lax.psum_scatter(keyval_term.astype(jnp.bfloat16), ('fsdp', 'context'), s...  65.4 us
    all_gather x1, waiting for transfers between devices, shards(): lax.all_gather(w_down, ('fsdp', 'context'), axis=0, tiled=True)  58.4 us
    psum x1, waiting for transfers between devices, shards(): branch = lax.psum(contract_last(mixed_low, out_all), 'tensor')  55.6 us
    psum x1, waiting for transfers between devices, shards(): lax.psum(d_normed_part.astype(jnp.bfloat16), 'tensor').astype(jnp.float32)  36.4 us
    psum x1, waiting for transfers between devices, shards(): lax.psum(contract_last(active, lax.all_gather(w_down, ('fsdp', 'context')...  35.7 us
  transfers between devices with their start and end apart: 15, of which 11 were waited for; matrix products, arithmetic and copies ran while one was open for 8% of the time, Pallas kernels for 0%

commit v1 on v0

--- a/solution.py
+++ b/solution.py
@@ -6,6 +6,25 @@
 HD = 256
 WINDOW = 512
 EPSILON = 1e-06
+
+
+def loops_mark(q_in, base_x):
+    comm_axis = ("fsdp", "context")
+    right_arr = lax.axis_size(comm_axis)
+    state_next, block_out, lower = (right_arr, lax.axis_index(comm_axis), q_in.shape[0])
+    blocks_here = [(to_i, (to_i + 1) % state_next) for to_i in range(state_next)]
+    views = [(to_i, (to_i - 1) % state_next) for to_i in range(state_next)]
+    item_now = state_next // 2
+    f_next = reached = q_in
+    opened = base_x(q_in, block_out * lower)
+    for w in range(1, item_now + 1):
+        f_next = lax.ppermute(f_next, comm_axis, blocks_here)
+        if w < state_next - item_now:
+            reached = lax.ppermute(reached, comm_axis, views)
+            field_out = base_x(reached, (block_out + w) % state_next * lower)
+            opened = opened + field_out
+        opened = opened + base_x(f_next, (block_out - w) % state_next * lower)
+    return opened
 
 
 def from_behind(block, axis, distance):
@@ -139,11 +158,14 @@
     normed_mlp_f, pre_mlp_back = jax.vjp(rms_norm, hidden, gains_f[2])
     normed_mlp = normed_mlp_f.astype(jnp.bfloat16)
     columns = normed_mlp
-    gate_up = jnp.einsum(
-        "bn,nkf->bkf",
-        columns,
-        lax.all_gather(w_gateup, ("fsdp", "context"), axis=0, tiled=True),
-        preferred_element_type=jnp.float32,
+    gate_up = loops_mark(
+        w_gateup,
+        lambda shard, start_2: jnp.einsum(
+            "bn,nkf->bkf",
+            lax.dynamic_slice_in_dim(columns, start_2, shard.shape[0], axis=1),
+            shard,
+            preferred_element_type=jnp.float32,
+        ),
     )
     active_f, glu_back = jax.vjp(glu, gate_up)
     active = active_f.astype(jnp.bfloat16)

time: 1380 us -> 1440 us (1.043)
  waiting for transfers between devices: 1040 us -> 974 us
  blocking collectives: 118 us -> 174 us
  matrix products: 74.4 us -> 125 us
  starting transfers between devices: 10.2 us -> 38.4 us
    psum x1, waiting for transfers between devices: 55.6 us -> 0.02 us  [shards(): branch = lax.psum(contract_last(mixed_low, out_all), 'tensor')]
    all_gather x1, waiting for transfers between devices: 58.4 us -> 7.28 us  [shards(): lax.all_gather(w_down, ('fsdp', 'context'), axis=0, tiled=True)]
    all_gather x1, blocking collectives: 27.2 us -> 76.2 us  [shards(): lax.all_gather(norm_gains, ('fsdp', 'context'), axis=1, tiled=True)]
    dot_general x1 -> x8, matrix products: 8.27 us -> 56.9 us  [shards(): jnp.einsum('bn,nkf->bkf', lax.dynamic_slice_in_dim(columns, start_2, shar...]
    ppermute x0 -> x7, waiting for transfers between devices: none -> 39.2 us  [the longest x4 35.2 us: loops_mark(): f_next = lax.ppermute(f_next, comm_axis, blocks_here)]
    ppermute x0 -> x7, starting transfers between devices: none -> 32.3 us  [the longest x4 21.3 us: loops_mark(): f_next = lax.ppermute(f_next, comm_axis, blocks_here)]
  transfers between devices with their start and end apart: 15 -> 22, of which waited for: 11 -> 14; matrix products, arithmetic and copies ran while one was open for 8% -> 13% of each run, Pallas kernels for 0% -> 0%
where the time goes in v1:
time: 1440 us; the launch traced here: 1430 us
  waiting for transfers between devices  974 us (68%)
  blocking collectives  174 us (12%)
  matrix products  125 us (9%)
  other arithmetic  55 us (4%)
  local copies, waits for them, and re-layouts  50.4 us (4%)
  starting transfers between devices  38.4 us (3%)
  between operations  16.4 us (1%)
    unnamed x15, waiting for transfers between devices  565 us
    all_gather x1, waiting for transfers between devices, shards(): lax.all_gather(w_gateup, ('fsdp', 'context'), axis=0, tiled=True)  108 us
    all_gather x1, blocking collectives, shards(): lax.all_gather(norm_gains, ('fsdp', 'context'), axis=1, tiled=True)  76.2 us
    reduce_scatter x1, waiting for transfers between devices, shards(): lax.psum_scatter(jnp.stack([contract_first(features, d_query_low), contra...  65.4 us
    reduce_scatter x1, waiting for transfers between devices, shards(): lax.psum_scatter(keyval_term.astype(jnp.bfloat16), ('fsdp', 'context'), s...  65.3 us
    dot_general x8, matrix products, shards(): jnp.einsum('bn,nkf->bkf', lax.dynamic_slice_in_dim(columns, start_2, shar...  56.9 us
    psum x1, waiting for transfers between devices, shards(): lax.psum(contract_last(active, lax.all_gather(w_down, ('fsdp', 'context')...  50 us
    all_gather x1, blocking collectives, shards(): lax.all_gather(w_out, ('fsdp', 'context'), axis=0, tiled=True)  39.7 us
  transfers between devices with their start and end apart: 22, of which 14 were waited for; matrix products, arithmetic and copies ran while one was open for 13% of the time, Pallas kernels for 0%

profile of v1, /device:TPU:0, one launch (start us, length us, event | category | flops | bytes accessed | tf_op | source)
XLA Modules:
  0.0 1432.6 jit_solution(10466160254566446963)
XLA Ops:
  18.0 76.2 %all-gather = bf16[8,144,4]{1,2,0:T(4,128)(2,1)S(1)} all-gather(bf16[1,144,4]{1,2,0:T(4,128)(2,1)} %bitcast.275), channel_id=1, replica_groups=mesh['fsdp'=2,'context'=4,'tensor'=4] {'fsdp','context'}, dimensions={0}, use_global_device_ids=true | all-gather | bytes 10368 | tf_op jit(solution)/shard_map/all_gather | solution.py:91
  94.3 18.4 %all-gather.1 = bf16[8,32,2]{1,2,0:T(2,128)(2,1)S(1)} all-gather(bf16[1,32,2]{1,2,0:T(2,128)(2,1)} %bitcast.276), channel_id=1, replica_groups=mesh['fsdp'=2,'context'=4,'tensor'=4] {'fsdp','context'}, dimensions={0}, use_global_device_ids=true | all-gather | bytes 1152 | tf_op jit(solution)/shard_map/all_gather | solution.py:92
  113.8 32.4 %all_gather.25 = bf16[1152,256]{1,0:T(8,128)(2,1)S(1)} all-gather(bf16[144,256]{1,0:T(8,128)(2,1)S(1)} %copy-done.39), channel_id=1, replica_groups=mesh['fsdp'=2,'context'=4,'tensor'=4] {'fsdp','context'}, dimensions={0}, use_global_device_ids=true | all-gather | bytes 663552 | tf_op jit(solution)/shard_map/all_gather | solution.py:93
  156.1 39.7 %all_gather.26 = bf16[1152,256]{1,0:T(8,128)(2,1)S(1)} all-gather(bf16[144,256]{1,0:T(8,128)(2,1)S(1)} %copy-done.40), channel_id=1, replica_groups=mesh['fsdp'=2,'context'=4,'tensor'=4] {'fsdp','context'}, dimensions={0}, use_global_device_ids=true | all-gather | bytes 663552 | tf_op jit(solution)/shard_map/all_gather | solution.py:95
  210.5 17.0 %collective-permute-done.5 = bf16[144,2,1728]{2,0,1:T(8,128)(2,1)} collective-permute-done((bf16[144,2,1728]{2,0,1:T(8,128)(2,1)}, bf16[144,2,1728]{2,0,1:T(8,128)(2,1)}, u32[]{:S(2)}, u32[]{:S(2)}) %collective-permute-start.5) | collective-permute-done | bytes 995360 | tf_op jit(solution)/shard_map/ppermute | solution.py:21
  227.5 17.7 %collective-permute-start.7 = (bf16[144,2,1728]{2,0,1:T(8,128)(2,1)}, bf16[144,2,1728]{2,0,1:T(8,128)(2,1)}, u32[]{:S(2)}, u32[]{:S(2)}) collective-permute-start(bf16[144,2,1728]{2,0,1:T(8,128)(2,1)} %collective-permute-done.5), channel_id=1, source_target_pairs={{0,4},{4,8},{8,12},{12,16},{16,20},{20,24},{24,28},{28,0},{1,5},{5... | collective-permute-start | bytes 2985992 | tf_op jit(solution)/shard_map/ppermute | solution.py:21
  251.5 18.2 %collective-permute-done.7 = bf16[144,2,1728]{2,0,1:T(8,128)(2,1)} collective-permute-done((bf16[144,2,1728]{2,0,1:T(8,128)(2,1)}, bf16[144,2,1728]{2,0,1:T(8,128)(2,1)}, u32[]{:S(2)}, u32[]{:S(2)}) %collective-permute-start.7) | collective-permute-done | bytes 995360 | tf_op jit(solution)/shard_map/ppermute | solution.py:21
  311.8 20.5 %add_add_fusion = f32[512,2,1728]{0,2,1:T(8,128)} fusion(f32[512,2,1728]{0,2,1:T(8,128)} %fusion.107, f32[512,2,1728]{0,2,1:T(8,128)} %fusion.109, f32[512,2,1728]{0,2,1:T(8,128)} %fusion.111, f32[512,2,1728]{0,2,1:T(8,128)} %fusion.113, f32[512,2,1728]{0,2,1:T(8,128)} %fusion.115, f32[512,2,1728]{0,2,1:T(8,128)} %fusion.119, f32[512,2,1728]{0,2,1:T(8,128)} %fusion.117, ...), kind=kOutput, calls=%fused_computation.4 | convolution fusion | flops 521994240 | bytes 57880580 | tf_op jit(solution)/shard_map/bn,nkf->bkf/dot_general | solution.py:163
  337.8 7.3 all-gather.8.cloned.1.call-done
  345.1 6.3 convolution_convert_fusion.4
  352.1 50.0 %all-reduce.17.cloned.1.call-done = bf16[512,1152]{1,0:T(8,128)(2,1)} async-done(((bf16[512,1152]{1,0:T(8,128)(2,1)}), bf16[512,1152]{1,0:T(8,128)(2,1)}) %all-reduce.17.cloned.1.call-update) | async-done | bytes 1179664 | tf_op jit(solution)/shard_map/psum | solution.py:172
  407.6 12.1 multiply_bitcast_fusion
  419.7 108.0 %all-gather.10.cloned.1.call-done = bf16[1152,2,1728]{2,0,1:T(8,128)(2,1)} async-done(((bf16[144,2,1728]{2,0,1:T(8,128)(2,1)}), bf16[1152,2,1728]{2,0,1:T(8,128)(2,1)}) %all-gather.10.cloned.1.call-update) | async-done | bytes 7962640 | tf_op jit(solution)/shard_map/all_gather | solution.py:193
  527.7 11.4 fusion.8
  540.4 34.5 %all-reduce.19.cloned.1.call-done = bf16[512,1152]{1,0:T(8,128)(2,1)} async-done(((bf16[512,1152]{1,0:T(8,128)(2,1)}), bf16[512,1152]{1,0:T(8,128)(2,1)}) %all-reduce.19.cloned.1.call-update) | async-done | bytes 1179664 | tf_op jit(solution)/shard_map/psum | solution.py:196
  595.1 10.4 collective-permute-done.9
  610.3 7.0 psum.47
  622.1 28.7 %all-reduce.23.cloned.1.call-done = (bf16[512,1152]{1,0:T(8,128)(2,1)}, bf16[512,512]{0,1:T(8,128)(2,1)}) async-done(((bf16[512,1152]{1,0:T(8,128)(2,1)}, bf16[512,512]{0,1:T(8,128)(2,1)}), (bf16[512,1152]{1,0:T(8,128)(2,1)}, bf16[512,512]{0,1:T(8,128)(2,1)})) %all-reduce.23.cloned.1.call-update) | async-done | bytes 1703952 | tf_op jit(solution)/shard_map/psum | solution.py:257
  670.9 9.1 convolution_convert_fusion
  685.3 27.0 %copy.79 = bf16[1152,3,1728]{2,1,0:T(4,128)(2,1)} copy(bf16[1152,3,1728]{0,2,1:T(8,128)(2,1)} %pad_maximum_fusion) | data formatting | bytes 23887872 | tf_op jit(solution)/shard_map/concatenate | solution.py:206
  719.7 60.7 %reduce-scatter.13.cloned.1.call-done = bf16[144,4]{1,0:T(8,128)(2,1)} async-done(((bf16[1152,4]{1,0:T(8,128)(2,1)}), bf16[144,4]{1,0:T(8,128)(2,1)}) %reduce-scatter.13.cloned.1.call-update) | async-done | bytes 1168
  781.9 65.4 %reduce-scatter.9.cloned.1.call-done = bf16[144,2,256]{2,0,1:T(8,128)(2,1)} async-done(((bf16[1152,2,256]{2,0,1:T(8,128)(2,1)}), bf16[144,2,256]{2,0,1:T(8,128)(2,1)}) %reduce-scatter.9.cloned.1.call-update) | async-done | bytes 147472 | tf_op jit(solution)/shard_map/reduce_scatter | solution.py:272
  849.0 65.3 %reduce-scatter.11.cloned.1.call-done = bf16[144,512]{1,0:T(8,128)(2,1)} async-done(((bf16[1152,512]{1,0:T(8,128)(2,1)}), bf16[144,512]{1,0:T(8,128)(2,1)}) %reduce-scatter.11.cloned.1.call-update) | async-done | bytes 147472 | tf_op jit(solution)/shard_map/reduce_scatter | solution.py:290
  915.9 503.4 %all-reduce.21.cloned.1.call-done = bf16[1152,3,1728]{2,1,0:T(4,128)(2,1)} async-done(((bf16[1152,3,1728]{2,1,0:T(4,128)(2,1)}), bf16[1152,3,1728]{2,1,0:T(4,128)(2,1)}) %all-reduce.21.cloned.1.call-update) | async-done | bytes 11943952
  (321 shorter events, 169.7 us)
Async XLA Ops:
  7.2 106.6 %copy-start.39 = (bf16[144,256]{1,0:T(8,128)(2,1)S(1)}, bf16[144,256]{1,0:T(8,128)(2,1)}, u32[]{:S(2)}) copy-start(bf16[144,256]{1,0:T(8,128)(2,1)} %param.20) | copy-start | bytes 221188
  7.2 141.4 %all-gather.6.cloned.1.call-start = ((), (), s32[]{:S(2)}) async-start(), calls=%async_computation.4 | async-start | bytes 1327104 | tf_op jit(solution)/shard_map/all_gather | solution.py:94
  8.7 138.2 %copy-start.22 = (bf16[144,2,1728]{2,0,1:T(8,128)(2,1)}, bf16[144,2,1728]{2,0,1:T(8,128)(2,1)S(1)}, u32[]{:S(2)}) copy-start(bf16[144,2,1728]{2,0,1:T(8,128)(2,1)S(1)} %copy.68) | copy-start | bytes 2985988
  8.7 198.9 %collective-permute-start.2 = (bf16[144,2,1728]{2,0,1:T(8,128)(2,1)S(1)}, bf16[144,2,1728]{2,0,1:T(8,128)(2,1)}, u32[]{:S(2)}, u32[]{:S(2)}) collective-permute-start(bf16[144,2,1728]{2,0,1:T(8,128)(2,1)S(1)} %copy.68), channel_id=1, source_target_pairs={{0,28},{4,0},{8,4},{12,8},{16,12},{20,16},{24,20},{28,24},{1,29},{... | collective-permute-start | bytes 2985992 | tf_op jit(solution)/shard_map/ppermute | solution.py:23
  14.7 182.5 %collective-permute-start.3 = (bf16[144,2,1728]{2,0,1:T(8,128)(2,1)S(1)}, bf16[144,2,1728]{2,0,1:T(8,128)(2,1)}, u32[]{:S(2)}, u32[]{:S(2)}) collective-permute-start(bf16[144,2,1728]{2,0,1:T(8,128)(2,1)S(1)} %copy.68), channel_id=1, source_target_pairs={{0,4},{4,8},{8,12},{12,16},{16,20},{20,24},{24,28},{28,0},{1,5},{5... | collective-permute-start | bytes 2985992 | tf_op jit(solution)/shard_map/ppermute | solution.py:21
  14.8 255.1 %all-reduce.15.cloned.1.call-start = ((), (), s32[]{:S(2)}) async-start(), calls=%async_computation.5 | async-start | bytes 4718592 | tf_op jit(solution)/shard_map/psum | solution.py:155
  16.1 179.7 %collective-permute-start.1 = (s32[2,512]{1,0:T(2,128)}, s32[2,512]{1,0:T(2,128)}, u32[]{:S(2)}, u32[]{:S(2)}) collective-permute-start(s32[2,512]{1,0:T(2,128)} %pad_add_fusion.2), channel_id=1, source_target_pairs={{0,4},{4,8},{8,12},{1,5},{5,9},{9,13},{2,6},{6,10},{10,14},{3,7},{... | collective-permute-start | bytes 12296 | tf_op jit(solution)/shard_map/ppermute | solution.py:33
  154.0 46.7 %collective-permute-start = (bf16[512,512]{0,1:T(8,128)(2,1)}, bf16[512,512]{0,1:T(8,128)(2,1)}, u32[]{:S(2)}, u32[]{:S(2)}) collective-permute-start(bf16[512,512]{0,1:T(8,128)(2,1)} %pad_maximum_fusion.3), channel_id=1, source_target_pairs={{0,4},{4,8},{8,12},{1,5},{5,9},{9,13},{2,6},{6,10},{10,14},{3,7},{... | collective-permute-start | bytes 1572872 | tf_op jit(solution)/shard_map/ppermute | solution.py:33
  197.3 30.2 %collective-permute-start.5 = (bf16[144,2,1728]{2,0,1:T(8,128)(2,1)}, bf16[144,2,1728]{2,0,1:T(8,128)(2,1)}, u32[]{:S(2)}, u32[]{:S(2)}) collective-permute-start(bf16[144,2,1728]{2,0,1:T(8,128)(2,1)} %collective-permute-done.3), channel_id=1, source_target_pairs={{0,4},{4,8},{8,12},{12,16},{16,20},{20,24},{24,28},{28,0},{1,5},{5... | collective-permute-start | bytes 2985992 | tf_op jit(solution)/shard_map/ppermute | solution.py:21
  207.6 137.5 %all-gather.8.cloned.1.call-start = ((), (), s32[]{:S(2)}) async-start(), calls=%async_computation.6 | async-start | bytes 4644864 | tf_op jit(solution)/shard_map/all_gather | solution.py:174
  207.6 41.8 %collective-permute-start.4 = (bf16[144,2,1728]{2,0,1:T(8,128)(2,1)}, bf16[144,2,1728]{2,0,1:T(8,128)(2,1)}, u32[]{:S(2)}, u32[]{:S(2)}) collective-permute-start(bf16[144,2,1728]{2,0,1:T(8,128)(2,1)} %collective-permute-done.2), channel_id=1, source_target_pairs={{0,28},{4,0},{8,4},{12,8},{16,12},{20,16},{24,20},{28,24},{1,29},{... | collective-permute-start | bytes 2985992 | tf_op jit(solution)/shard_map/ppermute | solution.py:23
  227.5 42.2 %collective-permute-start.7 = (bf16[144,2,1728]{2,0,1:T(8,128)(2,1)}, bf16[144,2,1728]{2,0,1:T(8,128)(2,1)}, u32[]{:S(2)}, u32[]{:S(2)}) collective-permute-start(bf16[144,2,1728]{2,0,1:T(8,128)(2,1)} %collective-permute-done.5), channel_id=1, source_target_pairs={{0,4},{4,8},{8,12},{12,16},{16,20},{20,24},{24,28},{28,0},{1,5},{5... | collective-permute-start | bytes 2985992 | tf_op jit(solution)/shard_map/ppermute | solution.py:21
  245.3 156.9 %all-reduce.17.cloned.1.call-start = ((), (), s32[]{:S(2)}) async-start(), calls=%async_computation.7 | async-start | bytes 2359296 | tf_op jit(solution)/shard_map/psum | solution.py:172
  249.4 56.8 %collective-permute-start.6 = (bf16[144,2,1728]{2,0,1:T(8,128)(2,1)}, bf16[144,2,1728]{2,0,1:T(8,128)(2,1)}, u32[]{:S(2)}, u32[]{:S(2)}) collective-permute-start(bf16[144,2,1728]{2,0,1:T(8,128)(2,1)} %collective-permute-done.4), channel_id=1, source_target_pairs={{0,28},{4,0},{8,4},{12,8},{16,12},{20,16},{24,20},{28,24},{1,29},{... | collective-permute-start | bytes 2985992 | tf_op jit(solution)/shard_map/ppermute | solution.py:23
  269.7 42.0 %collective-permute-start.8 = (bf16[144,2,1728]{2,0,1:T(8,128)(2,1)}, bf16[144,2,1728]{2,0,1:T(8,128)(2,1)}, u32[]{:S(2)}, u32[]{:S(2)}) collective-permute-start(bf16[144,2,1728]{2,0,1:T(8,128)(2,1)} %collective-permute-done.7), channel_id=1, source_target_pairs={{0,4},{4,8},{8,12},{12,16},{16,20},{20,24},{24,28},{28,0},{1,5},{5... | collective-permute-start | bytes 2985992 | tf_op jit(solution)/shard_map/ppermute | solution.py:21
  351.4 176.2 %all-gather.10.cloned.1.call-start = ((), (), s32[]{:S(2)}) async-start(), calls=%async_computation.8 | async-start | bytes 9289728 | tf_op jit(solution)/shard_map/all_gather | solution.py:193
  352.0 222.9 %all-reduce.19.cloned.1.call-start = ((), (), s32[]{:S(2)}) async-start(), calls=%async_computation.9 | async-start | bytes 2359296 | tf_op jit(solution)/shard_map/psum | solution.py:196
  539.1 111.7 %all-reduce.23.cloned.1.call-start = ((), (), s32[]{:S(2)}) async-start(), calls=%async_computation.15 | async-start | bytes 3407872 | tf_op jit(solution)/shard_map/psum | solution.py:257
  590.0 15.5 %collective-permute-start.9 = (bf16[512,512]{0,1:T(8,128)(2,1)S(1)}, bf16[512,512]{0,1:T(8,128)(2,1)S(1)}, u32[]{:S(2)}, u32[]{:S(2)}) collective-permute-start(bf16[512,512]{0,1:T(8,128)(2,1)S(1)} %fusion.62), channel_id=1, source_target_pairs={{4,0},{8,4},{12,8},{5,1},{9,5},{13,9},{6,2},{10,6},{14,10},{7,3},{... | collective-permute-start | bytes 1572872 | tf_op jit(solution)/shard_map/ppermute | solution.py:33
  606.4 111.9 %reduce-scatter.15.cloned.1.call-start = ((), (), s32[]{:S(2)}) async-start(), calls=%async_computation.13 | async-start | bytes 73728
  655.6 124.8 %reduce-scatter.13.cloned.1.call-start = ((), (), s32[]{:S(2)}) async-start(), calls=%async_computation.12 | async-start | bytes 331776
  661.9 185.4 %reduce-scatter.9.cloned.1.call-start = ((), (), s32[]{:S(2)}) async-start(), calls=%async_computation.10 | async-start | bytes 1327104 | tf_op jit(solution)/shard_map/reduce_scatter | solution.py:272
  663.2 251.1 %reduce-scatter.11.cloned.1.call-start = ((), (), s32[]{:S(2)}) async-start(), calls=%async_computation.11 | async-start | bytes 1327104 | tf_op jit(solution)/shard_map/reduce_scatter | solution.py:290
  666.4 752.9 %all-reduce.21.cloned.1.call-start = ((), (), s32[]{:S(2)}) async-start(), calls=%async_computation.14 | async-start | bytes 33030144
  (85 other events, 1083.5 us)
Sparse Core Ops, SparseCore 0:
  14.9 58.7 all-gather.5
  207.7 55.5 all-reduce.14
  265.4 79.5 all-gather.7
  351.6 50.5 all-reduce.16
  404.7 122.9 all-gather.9
  539.2 35.6 all-reduce.18
  606.6 44.1 all-reduce.22
  655.8 62.5 reduce-scatter.14
  722.2 58.1 reduce-scatter.12
  783.6 63.6 reduce-scatter.8
  850.7 63.5 reduce-scatter.10
  918.2 501.0 all-reduce.20
